TPU v7x, 32 devices: a whole 2x2x4 slice. The times are simulated.
32 devices in a mesh: row: 4 (over y, core), col: 8 (over z, x).
Axes of the slice: x: 2, y: 2, z: 4, core: 2. Of those that a mesh axis runs over, the one named last changes fastest.
Arguments:
- vectors: bfloat16 [4, 8, 128, 384], P('row', 'col'), may hold values from -6 to 6
- near_blocks: bfloat16 [4, 8, 9, 384, 384], P('row', 'col'), may hold values from -0.15625 to 0.15625
- near_source: int32 [4, 8, 9], P('row', 'col'), may hold values from 0 to 8, each once within a row
- near_count: int32 [4, 8], P('row', 'col'), may hold values from 1 to 9
- basis_col: bfloat16 [4, 8, 64, 384], P('row', 'col'), may hold values from -0.3125 to 0.3125
- transfer_col: bfloat16 [4, 8, 64, 64], P('row', 'col'), may hold values from -0.25 to 0.25
- leaf_couple: bfloat16 [4, 8, 3, 5, 64, 64], P('row', 'col'), may hold values from -0.1875 to 0.1875
- coupling: bfloat16 [4, 4, 64, 64], P('row'), may hold values from -0.75 to 0.75
- distant_region_list: int32 [4, 4], P('row'), may hold values from 0 to 3, each once within a row
- transfer_row: bfloat16 [4, 8, 64, 64], P('row', 'col'), may hold values from -0.75 to 0.75
- basis_row: bfloat16 [4, 8, 64, 384], P('row', 'col'), may hold values from -0.75 to 0.75
Outputs:
- product: bfloat16 [4, 8, 128, 384], P('row', 'col')
Inputs may be any that keep to these rules, and one draw needn't show every extreme that they name: `near_source`: the 9 slots of a leaf name the nine neighbourhood cells once each. Only the first near_count slots of a leaf are live. `distant_region_list`: each region's list names every region once.
All inputs are finite; a program needn't handle non-finite values.
Results may differ from a plain program's by a relative error of at most 0.013.
Values may be sent and summed in bfloat16 or wider, within the bound.
A program may use at most 64 MiB of HBM per device.

v0:
```python
import functools

import jax
import jax.numpy as jnp
from jax import lax
from jax.experimental import pallas as pl
from jax.experimental.pallas import tpu as pltpu
from jax.sharding import PartitionSpec as P

REACH = 3
MESH = pl.DeviceIdType.MESH
BF16 = jnp.bfloat16
F32 = jnp.float32


def dot(a, b, dims):
    return lax.dot_general(a, b, (dims, ((), ())), preferred_element_type=F32)


def kernel(
    rows,
    cols,
    source_ref,
    count_ref,
    list_ref,
    vectors_hbm,
    blocks_hbm,
    basis_col_hbm,
    transfer_col_hbm,
    couple_hbm,
    coupling_hbm,
    transfer_row_hbm,
    basis_row_hbm,
    out_ref,
    table,
    blocks,
    basis_col,
    transfer_col,
    couple,
    coupling,
    transfer_row,
    basis_row,
    leaf_send,
    up_send,
    reduced_send,
    leaf_buf,
    chunk_buf,
    region_buf,
    local_sems,
    near_send_sems,
    near_recv_sems,
    group_sems,
):
    r, c = lax.axis_index("row"), lax.axis_index("col")
    band = cols - REACH

    def behind(d, e):
        return (lax.rem(r + rows - d, rows), lax.rem(c + cols - e, cols))

    barrier = pltpu.get_barrier_semaphore()
    if rows * cols <= 64:
        for k in range(1, rows * cols):
            pl.semaphore_signal(barrier, inc=1, device_id=behind(k // cols, k % cols), device_id_type=MESH)
    else:

        @pl.loop(1, rows * cols)
        def _(k):
            pl.semaphore_signal(
                barrier, inc=1, device_id=behind(k // cols, lax.rem(k, cols)), device_id_type=MESH
            )

    loads = [
        pltpu.make_async_copy(src, dst, local_sems.at[i])
        for i, (src, dst) in enumerate(
            [
                (vectors_hbm, table.at[0]),
                (basis_col_hbm, basis_col),
                (transfer_col_hbm, transfer_col),
                (blocks_hbm, blocks),
                (couple_hbm, couple),
                (coupling_hbm, coupling),
                (transfer_row_hbm, transfer_row),
                (basis_row_hbm, basis_row),
            ]
        )
    ]
    for load in loads:
        load.start()
    for load in loads[:3]:
        load.wait()
    leaf_low = dot(basis_col[...], table[0], ((1,), (1,))).astype(BF16)
    leaf_send[...] = leaf_low
    up = dot(transfer_col[...], leaf_low, ((0,), (0,))).astype(BF16)
    chunk = up_send.shape[1]
    for e in range(cols):
        up_send[e] = up[e * chunk : (e + 1) * chunk]

    pl.semaphore_wait(barrier, rows * cols - 1)

    def remote(src, dst, send_sem, recv_sem, target):
        return pltpu.make_async_remote_copy(
            src_ref=src, dst_ref=dst, send_sem=send_sem, recv_sem=recv_sem,
            device_id=target, device_id_type=MESH,
        )

    parity = lax.rem(r, 2)
    partner = (r + 1 - 2 * parity, c)
    odd, even = parity == 1, parity == 0

    for e in range(1, cols):
        remote(
            up_send.at[lax.rem(c + cols - e, cols)], chunk_buf.at[e], group_sems.at[0], group_sems.at[1], behind(0, e)
        ).start()
    own_band = leaf_buf.at[pl.ds(0, band)]
    mid_band = leaf_buf.at[pl.ds(band, band)]
    top_band = leaf_buf.at[pl.ds(2 * band, band)]
    for j in range(band):
        remote(leaf_send, leaf_buf.at[j], group_sems.at[2], group_sems.at[3], behind(0, REACH + j)).start()
    near = {}
    for d, e in ((2, 0), (0, 2), (0, 1), (2, 1), (2, 2)):
        cell = d * REACH + e
        near[cell] = remote(
            table.at[0], table.at[cell], near_send_sems.at[cell], near_recv_sems.at[cell], behind(d, e)
        )
        near[cell].start()
    for e in range(REACH):
        cell = REACH + e
        near[cell] = remote(
            table.at[2 * REACH * (1 - parity) + e],
            table.at[cell],
            near_send_sems.at[cell],
            near_recv_sems.at[cell],
            partner,
        )
    band_up = remote(own_band, top_band, group_sems.at[4], group_sems.at[5], behind(2, 0))
    band_across = remote(
        leaf_buf.at[pl.ds(2 * band * (1 - parity), band)], mid_band, group_sems.at[6], group_sems.at[7], partner
    )

    def start_if(condition, copy):
        @pl.when(condition)
        def _():
            copy.start()

    start_if(odd, near[REACH])
    for load in loads[3:]:
        load.wait()

    count = count_ref[0, 0]

    def term(cell):
        slot = jnp.int32(0)
        for s in range(source_ref.shape[0]):
            slot = jnp.where(source_ref[s] == cell, s, slot)
        source = table[cell]
        source = jnp.where(slot < count, source, jnp.zeros_like(source))
        return dot(source, blocks[slot], ((1,), (0,)))

    arrived = chunk_buf.at[pl.ds(1, cols - 1)]
    pltpu.make_async_copy(arrived, arrived, group_sems.at[1]).wait()
    reduced = up_send[c].astype(F32)
    for e in range(1, cols):
        reduced = reduced + chunk_buf[e].astype(F32)
    reduced_send[...] = reduced.astype(BF16)
    pltpu.make_async_copy(own_band, own_band, group_sems.at[3]).wait()
    band_up.start()
    start_if(odd, band_across)
    total = term(0)
    for d in range(REACH, rows):
        for e in range(cols):
            remote(
                reduced_send, region_buf.at[d - REACH, c], group_sems.at[8], group_sems.at[9], behind(d, e)
            ).start()

    near[2 * REACH].wait_recv()
    start_if(even, near[REACH])
    total = total + term(2 * REACH)
    band_up.wait_recv()
    start_if(even, band_across)
    for e in (2, 1):
        near[e].wait_recv()
        start_if(odd, near[REACH + e])
        total = total + term(e)
    near[REACH].wait_recv()
    total = total + term(REACH)

    pltpu.make_async_copy(region_buf, region_buf, group_sems.at[9]).wait()
    rank, vecs = leaf_buf.shape[1:]
    region_out = None
    for d in range(REACH, rows):
        target = lax.rem(r + d, rows)
        slot = jnp.int32(0)
        for f in range(rows):
            slot = jnp.where(list_ref[f] == target, f, slot)
        region = region_buf[d - REACH].astype(F32).reshape(rank, vecs).astype(BF16)
        part = dot(coupling[slot], region, ((0,), (0,)))
        region_out = part if region_out is None else region_out + part
    leaf_out = dot(transfer_row[...], region_out.astype(BF16), ((0,), (0,)))
    band_across.wait_recv()
    leaf_out = leaf_out + dot(
        couple[...].reshape(REACH * band * rank, rank),
        leaf_buf[...].reshape(REACH * band * rank, vecs),
        ((0,), (0,)),
    )
    total = total + dot(leaf_out.astype(BF16), basis_row[...], ((0,), (0,)))

    for e in (1, 2):
        near[2 * REACH + e].wait_recv()
        start_if(even, near[REACH + e])
        total = total + term(2 * REACH + e)
    for e in (1, 2):
        near[REACH + e].wait_recv()
        total = total + term(REACH + e)
    out_ref[...] = total.astype(out_ref.dtype)

    for copy in near.values():
        copy.wait_send()
    band_up.wait_send()
    band_across.wait_send()
    pltpu.make_async_copy(arrived, arrived, group_sems.at[0]).wait()
    pltpu.make_async_copy(own_band, own_band, group_sems.at[2]).wait()
    pltpu.make_async_copy(region_buf, region_buf, group_sems.at[8]).wait()


def per_device(
    vectors,
    near_blocks,
    near_source,
    near_count,
    basis_col,
    transfer_col,
    leaf_couple,
    coupling,
    distant_region_list,
    transfer_row,
    basis_row,
):
    rows, cols = lax.axis_size("row"), lax.axis_size("col")
    vecs, leaf = vectors.shape[2:]
    rank = basis_col.shape[2]
    cells = near_blocks.shape[2]
    band = leaf_couple.shape[3]
    smem = pl.BlockSpec(memory_space=pltpu.SMEM)
    hbm = pl.BlockSpec(memory_space=pl.ANY)
    out = pl.pallas_call(
        functools.partial(kernel, rows, cols),
        out_shape=jax.ShapeDtypeStruct((vecs, leaf), BF16),
        in_specs=[smem] * 3 + [hbm] * 8,
        out_specs=pl.BlockSpec(memory_space=pltpu.VMEM),
        scratch_shapes=[
            pltpu.VMEM((cells, vecs, leaf), BF16),
            pltpu.VMEM((cells, leaf, leaf), BF16),
            pltpu.VMEM((rank, leaf), BF16),
            pltpu.VMEM((rank, rank), BF16),
            pltpu.VMEM((REACH * band, rank, rank), BF16),
            pltpu.VMEM((rows, rank, rank), BF16),
            pltpu.VMEM((rank, rank), BF16),
            pltpu.VMEM((rank, leaf), BF16),
            pltpu.VMEM((rank, vecs), BF16),
            pltpu.VMEM((cols, rank // cols, vecs), BF16),
            pltpu.VMEM((rank // cols, vecs), BF16),
            pltpu.VMEM((REACH * band, rank, vecs), BF16),
            pltpu.VMEM((cols, rank // cols, vecs), BF16),
            pltpu.VMEM((rows - REACH, cols, rank // cols, vecs), BF16),
            pltpu.SemaphoreType.DMA((8,)),
            pltpu.SemaphoreType.DMA((cells,)),
            pltpu.SemaphoreType.DMA((cells,)),
            pltpu.SemaphoreType.DMA((10,)),
        ],
        compiler_params=pltpu.CompilerParams(collective_id=0, has_side_effects=True),
    )(
        near_source[0, 0],
        near_count,
        distant_region_list[0],
        vectors[0, 0],
        near_blocks[0, 0],
        basis_col[0, 0],
        transfer_col[0, 0],
        leaf_couple[0, 0].reshape(REACH * band, rank, rank),
        coupling[0],
        transfer_row[0, 0],
        basis_row[0, 0],
    )
    return out[None, None]


def solution(mesh):
    placed = (
        P("row", "col", None, None),
        P("row", "col", None, None, None),
        P("row", "col", None),
        P("row", "col"),
        P("row", "col", None, None),
        P("row", "col", None, None),
        P("row", "col", None, None, None, None),
        P("row", None, None, None),
        P("row", None),
        P("row", "col", None, None),
        P("row", "col", None, None),
    )
    return jax.shard_map(
        per_device,
        mesh=mesh,
        in_specs=placed,
        out_specs=P("row", "col", None, None),
        check_vma=False,
    )
```

profile of v0, /device:TPU:1, one launch (start us, length us, event | category | flops | bytes accessed | tf_op | source)
XLA Modules:
  0.0 25.4 jit_solution(9107940906880863990)
XLA Ops:
  0.7 23.2 %shard_map.109 = bf16[128,384]{1,0:T(8,128)(2,1)} custom-call(s32[9]{0:T(128)} %bitcast.20, s32[1,1]{1,0:T(1,128)S(6)} %copy.13.count_ref, s32[4]{0:T(128)} %bitcast.21, bf16[128,384]{1,0:T(8,128)(2,1)} %bitcast.14, bf16[9,384,384]{2,1,0:T(8,128)(2,1)} %bitcast.11, bf16[64,384]{1,0:T(8,128)(2,1)} %bitcast.16, bf16[64,64]{1,0:T(8,128)(2,1)} %bitcast.18, ...), custom_call_target="tpu_custom_call" | custom-call | tf_op jit(solution)/shard_map/pallas_call | solution.py:245
  23.9 1.5 %copy.14 = bf16[1,1,128,384]{3,2,1,0:T(8,128)(2,1)} copy(bf16[1,1,128,384]{3,2,1,0:T(8,128)(2,1)} %bitcast.12) | data formatting | bytes 196608
where the time goes:
time: 25.6 us; the launch traced here: 25.4 us
  Pallas kernels  23.2 us (91%)
  local copies, waits for them, and re-layouts  1.54 us (6%)
  between operations  0.66 us (3%)
    pallas_call x1, Pallas kernels, per_device(): pl.pallas_call(functools.partial(kernel, rows, cols), out_shape=jax.Shape...  23.2 us
    unnamed x1, local copies, waits for them, and re-layouts  1.54 us

commit v1 on v0

--- a/solution.py
+++ b/solution.py
@@ -20,9 +20,9 @@
 def kernel(
     rows,
     cols,
-    source_ref,
-    count_ref,
-    list_ref,
+    source_hbm,
+    count_hbm,
+    list_hbm,
     vectors_hbm,
     blocks_hbm,
     basis_col_hbm,
@@ -32,6 +32,9 @@
     transfer_row_hbm,
     basis_row_hbm,
     out_ref,
+    source_ref,
+    count_ref,
+    list_ref,
     table,
     blocks,
     basis_col,
@@ -81,6 +84,9 @@
                 (coupling_hbm, coupling),
                 (transfer_row_hbm, transfer_row),
                 (basis_row_hbm, basis_row),
+                (source_hbm, source_ref),
+                (count_hbm, count_ref),
+                (list_hbm, list_ref),
             ]
         )
     ]
@@ -240,14 +246,16 @@
     rank = basis_col.shape[2]
     cells = near_blocks.shape[2]
     band = leaf_couple.shape[3]
-    smem = pl.BlockSpec(memory_space=pltpu.SMEM)
     hbm = pl.BlockSpec(memory_space=pl.ANY)
     out = pl.pallas_call(
         functools.partial(kernel, rows, cols),
-        out_shape=jax.ShapeDtypeStruct((vecs, leaf), BF16),
-        in_specs=[smem] * 3 + [hbm] * 8,
+        out_shape=pltpu.VMEM((vecs, leaf), BF16),
+        in_specs=[hbm] * 11,
         out_specs=pl.BlockSpec(memory_space=pltpu.VMEM),
         scratch_shapes=[
+            pltpu.SMEM((cells,), jnp.int32),
+            pltpu.SMEM((1, 1), jnp.int32),
+            pltpu.SMEM((rows,), jnp.int32),
             pltpu.VMEM((cells, vecs, leaf), BF16),
             pltpu.VMEM((cells, leaf, leaf), BF16),
             pltpu.VMEM((rank, leaf), BF16),
@@ -262,7 +270,7 @@
             pltpu.VMEM((REACH * band, rank, vecs), BF16),
             pltpu.VMEM((cols, rank // cols, vecs), BF16),
             pltpu.VMEM((rows - REACH, cols, rank // cols, vecs), BF16),
-            pltpu.SemaphoreType.DMA((8,)),
+            pltpu.SemaphoreType.DMA((11,)),
             pltpu.SemaphoreType.DMA((cells,)),
             pltpu.SemaphoreType.DMA((cells,)),
             pltpu.SemaphoreType.DMA((10,)),

time: 25.6 us -> 23.4 us (0.914)
  Pallas kernels: 23.2 us -> 21.9 us
  local copies, waits for them, and re-layouts: 1.54 us -> 0.64 us
    pallas_call x1, Pallas kernels: 23.2 us -> 21.9 us  [per_device(): pl.pallas_call(functools.partial(kernel, rows, cols), out_shape=pltpu.VME...]
    unnamed x1, local copies, waits for them, and re-layouts: 1.54 us -> 0.64 us
where the time goes in v1:
time: 23.4 us; the launch traced here: 23.2 us
  Pallas kernels  21.9 us (94%)
  between operations  0.66 us (3%)
  local copies, waits for them, and re-layouts  0.64 us (3%)
    pallas_call x1, Pallas kernels, per_device(): pl.pallas_call(functools.partial(kernel, rows, cols), out_shape=pltpu.VME...  21.9 us
    unnamed x1, local copies, waits for them, and re-layouts  0.64 us

profile of v1, /device:TPU:1, one launch (start us, length us, event | category | flops | bytes accessed | tf_op | source)
XLA Modules:
  0.0 23.2 jit_solution(13332743593794387834)
XLA Ops:
  0.7 21.9 %shard_map.109 = bf16[128,384]{1,0:T(8,128)(2,1)S(1)} custom-call(s32[9]{0:T(128)} %bitcast.20, s32[1,1]{1,0:T(1,128)S(6)} %copy.14.count_hbm, s32[4]{0:T(128)} %bitcast.21, bf16[128,384]{1,0:T(8,128)(2,1)} %bitcast.14, bf16[9,384,384]{2,1,0:T(8,128)(2,1)} %bitcast.12, bf16[64,384]{1,0:T(8,128)(2,1)} %bitcast.16, bf16[64,64]{1,0:T(8,128)(2,1)} %bitcast.18, ...), custom_call_target="tpu_custom_call" | custom-call | tf_op jit(solution)/shard_map/pallas_call | solution.py:250
  22.6 0.6 %copy.13 = bf16[1,1,128,384]{3,2,1,0:T(8,128)(2,1)} copy(bf16[1,1,128,384]{3,2,1,0:T(8,128)(2,1)S(1)} %bitcast.11) | data formatting | bytes 196608

commit v2 on v1

v2 whole, which is shorter than its diff:
```python
import functools

import jax
import jax.numpy as jnp
from jax import lax
from jax.experimental import pallas as pl
from jax.experimental.pallas import tpu as pltpu
from jax.sharding import PartitionSpec as P

REACH = 3
PIECES = 2
MESH = pl.DeviceIdType.MESH
BF16 = jnp.bfloat16
F32 = jnp.float32


def dot(a, b, dims):
    return lax.dot_general(a, b, (dims, ((), ())), preferred_element_type=F32)


def kernel(
    rows,
    cols,
    source_hbm,
    count_hbm,
    list_hbm,
    vectors_hbm,
    blocks_hbm,
    basis_col_hbm,
    transfer_col_hbm,
    couple_hbm,
    coupling_hbm,
    transfer_row_hbm,
    basis_row_hbm,
    out_ref,
    source_ref,
    count_ref,
    list_ref,
    table,
    blocks,
    basis_col,
    transfer_col,
    couple,
    coupling,
    transfer_row,
    basis_row,
    leaf_send,
    up_send,
    reduced_send,
    leaf_buf,
    chunk_buf,
    region_buf,
    local_sems,
    near_send_sems,
    near_recv_sems,
    own_sems,
    up_send_sems,
    up_recv_sems,
    across_send_sems,
    across_recv_sems,
    group_sems,
    near_sem,
    far_sem,
):
    r, c = lax.axis_index("row"), lax.axis_index("col")
    parity = lax.rem(r, 2)
    band = cols - REACH
    near_reach = REACH - 1
    n_red, chunk = up_send.shape[0], up_send.shape[1]
    first_red = (cols - n_red) // 2
    is_red = jnp.logical_and(c >= first_red, c < first_red + n_red)

    def behind(d, e):
        return (lax.rem(r + rows - d, rows), lax.rem(c + cols - e, cols))

    def when(condition, act):
        @pl.when(condition)
        def _():
            act()

    loads = [
        pltpu.make_async_copy(src, dst, local_sems.at[i])
        for i, (src, dst) in enumerate(
            [
                (vectors_hbm, table.at[0]),
                (basis_col_hbm, basis_col),
                (transfer_col_hbm, transfer_col),
                (blocks_hbm, blocks),
                (couple_hbm, couple),
                (coupling_hbm, coupling),
                (transfer_row_hbm, transfer_row),
                (basis_row_hbm, basis_row),
                (source_hbm, source_ref),
                (count_hbm, count_ref),
                (list_hbm, list_ref),
            ]
        )
    ]
    for load in loads[:3]:
        load.start()

    barrier = pltpu.get_barrier_semaphore()

    def greet(sem, e, row_from=0, row_to=rows, row_not=rows):
        def one(row):
            pl.semaphore_signal(sem, inc=1, device_id=(row, lax.rem(c + cols - e, cols)), device_id_type=MESH)

        if rows <= 4:
            for row in range(rows):
                if isinstance(row_from, int) and isinstance(row_to, int):
                    one(row)
                else:
                    wanted = jnp.logical_and(row >= row_from, row < row_to)
                    when(jnp.logical_and(wanted, row != row_not), functools.partial(one, row))
        else:

            @pl.loop(row_from, row_to)
            def _(row):
                when(row != row_not, functools.partial(one, row))

    def greet_columns(low, high, condition, sem):
        if cols <= 8:
            for e in range(low, high):
                when(condition(e), functools.partial(greet, sem, e))
        else:

            @pl.loop(low, high)
            def _(e):
                when(condition(e), functools.partial(greet, sem, e))

    greet(barrier, 0, r + 1 - parity * 2, rows, r)
    greet_columns(1, cols, lambda e: c < e, barrier)

    for load in loads[3:]:
        load.start()
    for load in loads[:3]:
        load.wait()
    leaf_low = dot(basis_col[...], table[0], ((1,), (1,))).astype(BF16)
    leaf_send[...] = leaf_low
    up = dot(transfer_col[...], leaf_low, ((0,), (0,))).astype(BF16)
    for j in range(n_red):
        up_send[j] = up[j * chunk : (j + 1) * chunk]

    def remote(src, dst, send_sem, recv_sem, target):
        return pltpu.make_async_remote_copy(
            src_ref=src, dst_ref=dst, send_sem=send_sem, recv_sem=recv_sem,
            device_id=target, device_id_type=MESH,
        )

    side = lax.rem(c, 2)
    passes, direct = side == 0, side == 1
    partner = (r + 1 - 2 * parity, c)
    odd, even = parity == 1, parity == 0
    group = -(-band // up_send_sems.shape[0])
    spans = [(j, min(group, band - j)) for j in range(0, band, group)]

    pieces = near_send_sems.shape[1]
    part = table.shape[1] // pieces

    def near_copies(source, cell, target):
        return [
            remote(
                table.at[source, pl.ds(p * part, part)], table.at[cell, pl.ds(p * part, part)],
                near_send_sems.at[cell, p], near_recv_sems.at[cell, p], target,
            )
            for p in range(pieces)
        ]

    near = {}
    for d, e in ((2, 0), (0, 2), (2, 2)):
        near[d * REACH + e] = near_copies(0, d * REACH + e, behind(d, e))
    for d in (0, 2):
        cell = d * REACH + 1
        row, col = behind(d, 1)
        near[cell] = near_copies(
            (cell + 1) * (1 - side), cell, (jnp.where(passes, r, row), jnp.where(passes, c + 1, col))
        )
    for e in range(REACH):
        near[REACH + e] = near_copies(2 * REACH * (1 - parity) + e, REACH + e, partner)
    chunks = [
        remote(
            up_send.at[j],
            chunk_buf.at[lax.rem(c + cols - (first_red + j), cols)],
            group_sems.at[0],
            group_sems.at[1],
            (r, first_red + j),
        )
        for j in range(n_red)
    ]
    leaves = [
        remote(leaf_send, leaf_buf.at[j], group_sems.at[2], own_sems.at[j // group], behind(0, REACH + j))
        for j in range(band)
    ]
    band_up = [
        remote(
            leaf_buf.at[pl.ds(j, n)], leaf_buf.at[pl.ds(2 * band + j, n)],
            up_send_sems.at[j // group], up_recv_sems.at[j // group], behind(2, 0),
        )
        for j, n in spans
    ]
    band_across = [
        remote(
            leaf_buf.at[pl.ds(2 * band * (1 - parity) + j, n)], leaf_buf.at[pl.ds(band + j, n)],
            across_send_sems.at[j // group], across_recv_sems.at[j // group], partner,
        )
        for j, n in spans
    ]

    def sends(stage):
        def column(e):
            return c >= e if stage == 0 else c < e

        for j in range(n_red):
            up_by = first_red + j - c
            if stage == 0:
                known = up_by < 0
            elif stage == 1:
                known = jnp.logical_and(up_by > 0, up_by <= near_reach)
            else:
                known = up_by > near_reach
            when(known, chunks[j].start)
        for j in range(band):
            e = REACH + j
            if stage != (1 if cols - e > near_reach else 2):
                when(column(e), leaves[j].start)
        if stage != 1:
            for d in (0, 2):
                for near_copy in near[d * REACH + 2]:
                    when(column(2), near_copy.start)
        if stage == 0:
            for d in (0, 2):
                for near_copy in near[d * REACH + 1]:
                    when(direct, near_copy.start)
        if stage != 2:
            below = r >= 2
            for near_copy in near[2 * REACH]:
                when(below if stage == 0 else jnp.logical_not(below), near_copy.start)

    higher = cols - 1 - c
    close = jnp.minimum(near_reach, higher)
    pl.semaphore_wait(barrier, r + rows * c + 1 - parity)
    greet(near_sem, 0, 0, r - parity)
    greet_columns(1, near_reach + 1, lambda e: c >= e, near_sem)
    greet_columns(near_reach + 1, cols, lambda e: c >= e, far_sem)
    sends(0)
    above = rows - 2 - r + parity + rows * close
    when(above > 0, lambda: pl.semaphore_wait(near_sem, above))
    sends(1)

    for near_copy in near[REACH]:
        when(odd, near_copy.start)
    for load in loads[3:]:
        load.wait()

    count = count_ref[0, 0]

    def term(cell):
        slot = jnp.int32(0)
        for s in range(source_ref.shape[0]):
            slot = jnp.where(source_ref[s] == cell, s, slot)
        source = table[cell]
        source = jnp.where(slot < count, source, jnp.zeros_like(source))
        return dot(source, blocks[slot], ((1,), (0,)))

    total = term(0)
    distant = rows * (higher - close)
    when(distant > 0, lambda: pl.semaphore_wait(far_sem, distant))
    sends(2)

    arrived = chunk_buf.at[pl.ds(1, cols - 1)]

    @pl.when(is_red)
    def _():
        pltpu.make_async_copy(arrived, arrived, group_sems.at[1]).wait()
        reduced = up_send[jnp.clip(c - first_red, 0, n_red - 1)].astype(F32)
        for e in range(1, cols):
            reduced = reduced + chunk_buf[e].astype(F32)
        reduced_send[...] = reduced.astype(BF16)
        for d in range(REACH, rows):
            for e in range(cols):
                remote(
                    reduced_send, region_buf.at[d - REACH, c - first_red], group_sems.at[4], group_sems.at[5],
                    behind(d, e),
                ).start()

    def got(d, e):
        cell = d * REACH + e
        for p in range(pieces):
            near[cell][p].wait_recv()
            if (d, e) != (0, 0):
                when(odd if d == 0 else even, near[REACH + e][p].start)
            if e == 2:
                when(passes, near[cell - 1][p].start)

    def own_groups(lo, hi):
        for g in range(lo, hi):
            j, n = spans[g]
            view = leaf_buf.at[pl.ds(j, n)]
            pltpu.make_async_copy(view, view, own_sems.at[g]).wait()
            band_up[g].start()
            when(odd, band_across[g].start)

    def here(cell):
        for near_copy in near[cell]:
            near_copy.wait_recv()
        return term(cell)

    own_groups(0, len(spans))
    got(0, 2)
    got(2, 2)
    got(2, 0)
    for g in range(len(spans)):
        band_up[g].wait_recv()
        when(even, band_across[g].start)
    for cell in (2 * REACH, 2, 2 * REACH + 2):
        total = total + term(cell)
    total = total + here(REACH)
    got(0, 1)
    total = total + term(1)

    pltpu.make_async_copy(region_buf, region_buf, group_sems.at[5]).wait()
    rank, vecs = leaf_buf.shape[1:]
    region_out = None
    for d in range(REACH, rows):
        target = lax.rem(r + d, rows)
        slot = jnp.int32(0)
        for f in range(rows):
            slot = jnp.where(list_ref[f] == target, f, slot)
        region = region_buf[d - REACH].astype(F32).reshape(rank, vecs).astype(BF16)
        product = dot(coupling[slot], region, ((0,), (0,)))
        region_out = product if region_out is None else region_out + product
    leaf_out = dot(transfer_row[...], region_out.astype(BF16), ((0,), (0,)))
    for g in range(len(spans)):
        band_across[g].wait_recv()
    leaf_out = leaf_out + dot(
        couple[...].reshape(REACH * band * rank, rank),
        leaf_buf[...].reshape(REACH * band * rank, vecs),
        ((0,), (0,)),
    )
    total = total + dot(leaf_out.astype(BF16), basis_row[...], ((0,), (0,)))
    got(2, 1)
    total = total + term(2 * REACH + 1)
    total = total + here(REACH + 2)
    total = total + here(REACH + 1)
    out_ref[...] = total.astype(out_ref.dtype)

    for copies in near.values():
        for copy in copies:
            copy.wait_send()
    for copy in band_up + band_across:
        copy.wait_send()

    own_band = leaf_buf.at[pl.ds(0, band)]
    pltpu.make_async_copy(own_band, own_band, group_sems.at[2]).wait()

    @pl.when(is_red)
    def _():
        others = up_send.at[pl.ds(1, n_red - 1)]
        pltpu.make_async_copy(others, others, group_sems.at[0]).wait()
        for d in range(REACH, rows):
            pltpu.make_async_copy(chunk_buf, chunk_buf, group_sems.at[4]).wait()

    @pl.when(jnp.logical_not(is_red))
    def _():
        pltpu.make_async_copy(up_send, up_send, group_sems.at[0]).wait()


def per_device(
    vectors,
    near_blocks,
    near_source,
    near_count,
    basis_col,
    transfer_col,
    leaf_couple,
    coupling,
    distant_region_list,
    transfer_row,
    basis_row,
):
    rows, cols = lax.axis_size("row"), lax.axis_size("col")
    vecs, leaf = vectors.shape[2:]
    rank = basis_col.shape[2]
    cells = near_blocks.shape[2]
    band = leaf_couple.shape[3]
    n_red = cols // 2
    groups = min(band, 5)
    groups = -(-band // -(-band // groups))
    hbm = pl.BlockSpec(memory_space=pl.ANY)
    out = pl.pallas_call(
        functools.partial(kernel, rows, cols),
        out_shape=pltpu.VMEM((vecs, leaf), BF16),
        in_specs=[hbm] * 11,
        out_specs=pl.BlockSpec(memory_space=pltpu.VMEM),
        scratch_shapes=[
            pltpu.SMEM((cells,), jnp.int32),
            pltpu.SMEM((1, 1), jnp.int32),
            pltpu.SMEM((rows,), jnp.int32),
            pltpu.VMEM((cells, vecs, leaf), BF16),
            pltpu.VMEM((cells, leaf, leaf), BF16),
            pltpu.VMEM((rank, leaf), BF16),
            pltpu.VMEM((rank, rank), BF16),
            pltpu.VMEM((REACH * band, rank, rank), BF16),
            pltpu.VMEM((rows, rank, rank), BF16),
            pltpu.VMEM((rank, rank), BF16),
            pltpu.VMEM((rank, leaf), BF16),
            pltpu.VMEM((rank, vecs), BF16),
            pltpu.VMEM((n_red, rank // n_red, vecs), BF16),
            pltpu.VMEM((rank // n_red, vecs), BF16),
            pltpu.VMEM((REACH * band, rank, vecs), BF16),
            pltpu.VMEM((cols, rank // n_red, vecs), BF16),
            pltpu.VMEM((rows - REACH, n_red, rank // n_red, vecs), BF16),
            pltpu.SemaphoreType.DMA((11,)),
            pltpu.SemaphoreType.DMA((cells, PIECES)),
            pltpu.SemaphoreType.DMA((cells, PIECES)),
            pltpu.SemaphoreType.DMA((groups,)),
            pltpu.SemaphoreType.DMA((groups,)),
            pltpu.SemaphoreType.DMA((groups,)),
            pltpu.SemaphoreType.DMA((groups,)),
            pltpu.SemaphoreType.DMA((groups,)),
            pltpu.SemaphoreType.DMA((6,)),
            pltpu.SemaphoreType.REGULAR,
            pltpu.SemaphoreType.REGULAR,
        ],
        compiler_params=pltpu.CompilerParams(collective_id=0, has_side_effects=True),
    )(
        near_source[0, 0],
        near_count,
        distant_region_list[0],
        vectors[0, 0],
        near_blocks[0, 0],
        basis_col[0, 0],
        transfer_col[0, 0],
        leaf_couple[0, 0].reshape(REACH * band, rank, rank),
        coupling[0],
        transfer_row[0, 0],
        basis_row[0, 0],
    )
    return out[None, None]


def solution(mesh):
    placed = (
        P("row", "col", None, None),
        P("row", "col", None, None, None),
        P("row", "col", None),
        P("row", "col"),
        P("row", "col", None, None),
        P("row", "col", None, None),
        P("row", "col", None, None, None, None),
        P("row", None, None, None),
        P("row", None),
        P("row", "col", None, None),
        P("row", "col", None, None),
    )
    return jax.shard_map(
        per_device,
        mesh=mesh,
        in_specs=placed,
        out_specs=P("row", "col", None, None),
        check_vma=False,
    )
```

time: 23.4 us -> 20.3 us (0.87)
  the two profiles are of different devices: /device:TPU:1 before, /device:TPU:27 now
where the time goes in v2:
time: 20.3 us; the launch traced here: 20.2 us
  Pallas kernels  18.9 us (93%)
  between operations  0.66 us (3%)
  local copies, waits for them, and re-layouts  0.64 us (3%)
    pallas_call x1, Pallas kernels, per_device(): pl.pallas_call(functools.partial(kernel, rows, cols), out_shape=pltpu.VME...  18.9 us
    unnamed x1, local copies, waits for them, and re-layouts  0.64 us

profile of v2, /device:TPU:27, one launch (start us, length us, event | category | flops | bytes accessed | tf_op | source)
XLA Modules:
  0.0 20.2 jit_solution(8267387043544627372)
XLA Ops:
  0.7 18.9 %shard_map.109 = bf16[128,384]{1,0:T(8,128)(2,1)S(1)} custom-call(s32[9]{0:T(128)} %bitcast.20, s32[1,1]{1,0:T(1,128)S(6)} %copy.14.count_hbm, s32[4]{0:T(128)} %bitcast.21, bf16[128,384]{1,0:T(8,128)(2,1)} %bitcast.14, bf16[9,384,384]{2,1,0:T(8,128)(2,1)} %bitcast.12, bf16[64,384]{1,0:T(8,128)(2,1)} %bitcast.16, bf16[64,64]{1,0:T(8,128)(2,1)} %bitcast.18, ...), custom_call_target="tpu_custom_call" | custom-call | tf_op jit(solution)/shard_map/pallas_call | solution.py:390
  19.5 0.6 %copy.13 = bf16[1,1,128,384]{3,2,1,0:T(8,128)(2,1)} copy(bf16[1,1,128,384]{3,2,1,0:T(8,128)(2,1)S(1)} %bitcast.11) | data formatting | bytes 196608

commit v3 on v2

--- a/solution.py
+++ b/solution.py
@@ -8,7 +8,7 @@
 from jax.sharding import PartitionSpec as P
 
 REACH = 3
-PIECES = 2
+PIECES = 4
 MESH = pl.DeviceIdType.MESH
 BF16 = jnp.bfloat16
 F32 = jnp.float32
@@ -51,23 +51,20 @@
     chunk_buf,
     region_buf,
     local_sems,
-    near_send_sems,
     near_recv_sems,
     own_sems,
-    up_send_sems,
     up_recv_sems,
-    across_send_sems,
-    across_recv_sems,
     group_sems,
     near_sem,
     far_sem,
+    region_sem,
 ):
     r, c = lax.axis_index("row"), lax.axis_index("col")
     parity = lax.rem(r, 2)
     band = cols - REACH
     near_reach = REACH - 1
     n_red, chunk = up_send.shape[0], up_send.shape[1]
-    first_red = (cols - n_red) // 2
+    first_red = n_red
     is_red = jnp.logical_and(c >= first_red, c < first_red + n_red)
 
     def behind(d, e):
@@ -101,38 +98,97 @@
 
     barrier = pltpu.get_barrier_semaphore()
 
-    def greet(sem, e, row_from=0, row_to=rows, row_not=rows):
-        def one(row):
-            pl.semaphore_signal(sem, inc=1, device_id=(row, lax.rem(c + cols - e, cols)), device_id_type=MESH)
-
-        if rows <= 4:
-            for row in range(rows):
-                if isinstance(row_from, int) and isinstance(row_to, int):
-                    one(row)
+    def place(row, col):
+        return ((row // 2 + col // 2 + lax.rem(col, 2)) * cols + col) * rows + row
+
+    mine = place(r, c)
+
+    def near_column(col):
+        return jnp.abs(col - c) <= near_reach
+
+    far_rows = rows - REACH
+    one = jnp.bool_(True)
+
+    def to_row(k):
+        return one, behind(0, k + 1)
+
+    def to_facing(k):
+        return one, behind(rows - 2 + 4 * k if rows > 4 else 2, 0)
+
+    def to_targets(k):
+        return is_red, behind(REACH + k // cols, k % cols)
+
+    def to_reducers(k):
+        return one, (lax.rem(r + REACH + k // n_red, rows), first_red + k % n_red)
+
+    kinds = [
+        (cols - 1, to_row, near_column),
+        (2 if rows > 4 else 1, to_facing, lambda col: one),
+        (far_rows * cols, to_targets, None),
+        (far_rows * n_red, to_reducers, None),
+    ]
+
+    def greet(sem, device):
+        pl.semaphore_signal(sem, inc=1, device_id=device, device_id_type=MESH)
+
+    def greet_all(down):
+        for number, which, is_near in kinds:
+
+            def act(k, which=which, is_near=is_near):
+                valid, device = which(k)
+                if not down:
+                    when(jnp.logical_and(valid, place(*device) > mine), functools.partial(greet, barrier, device))
+                    return
+                below = jnp.logical_and(valid, place(*device) < mine)
+                if is_near is None:
+                    if which is to_reducers:
+                        when(below, functools.partial(greet, region_sem, device))
+                    return
+                close = is_near(device[1])
+                when(jnp.logical_and(below, close), functools.partial(greet, near_sem, device))
+                when(jnp.logical_and(below, jnp.logical_not(close)), functools.partial(greet, far_sem, device))
+
+            if number <= 16:
+                for k in range(number):
+                    act(k)
+            else:
+                pl.loop(0, number)(act)
+
+    def count_all(numbers):
+        for number, which, is_near in kinds:
+
+            def add(k, numbers, which=which, is_near=is_near):
+                valid, device = which(k)
+                above = place(*device) > mine
+                no = jnp.logical_not(one)
+                if is_near is None:
+                    found = (jnp.logical_not(above), no, no, above if which is to_targets else no)
                 else:
-                    wanted = jnp.logical_and(row >= row_from, row < row_to)
-                    when(jnp.logical_and(wanted, row != row_not), functools.partial(one, row))
-        else:
-
-            @pl.loop(row_from, row_to)
-            def _(row):
-                when(row != row_not, functools.partial(one, row))
-
-    def greet_columns(low, high, condition, sem):
-        if cols <= 8:
-            for e in range(low, high):
-                when(condition(e), functools.partial(greet, sem, e))
-        else:
-
-            @pl.loop(low, high)
-            def _(e):
-                when(condition(e), functools.partial(greet, sem, e))
-
-    greet(barrier, 0, r + 1 - parity * 2, rows, r)
-    greet_columns(1, cols, lambda e: c < e, barrier)
+                    close = is_near(device[1])
+                    found = (
+                        jnp.logical_not(above),
+                        jnp.logical_and(above, close),
+                        jnp.logical_and(above, jnp.logical_not(close)),
+                        no,
+                    )
+                return tuple(n + jnp.where(jnp.logical_and(valid, f), 1, 0) for n, f in zip(numbers, found))
+
+            if number <= 16:
+                for k in range(number):
+                    numbers = add(k, numbers)
+            else:
+                numbers = lax.fori_loop(0, number, add, numbers)
+        return numbers
+
+    greet(barrier, (r + 1 - 2 * parity, c))
+    greet_all(False)
+    zero = jnp.int32(0)
+    n_below, n_near_above, n_far_above, n_region_above = count_all((jnp.int32(1), zero, zero, zero))
 
     for load in loads[3:]:
         load.start()
+    pl.semaphore_wait(barrier, n_below)
+    greet_all(True)
     for load in loads[:3]:
         load.wait()
     leaf_low = dot(basis_col[...], table[0], ((1,), (1,))).astype(BF16)
@@ -151,32 +207,35 @@
     passes, direct = side == 0, side == 1
     partner = (r + 1 - 2 * parity, c)
     odd, even = parity == 1, parity == 0
-    group = -(-band // up_send_sems.shape[0])
+    group = -(-band // own_sems.shape[0])
     spans = [(j, min(group, band - j)) for j in range(0, band, group)]
 
-    pieces = near_send_sems.shape[1]
+    pieces = near_recv_sems.shape[1]
     part = table.shape[1] // pieces
 
     def near_copies(source, cell, target):
         return [
             remote(
                 table.at[source, pl.ds(p * part, part)], table.at[cell, pl.ds(p * part, part)],
-                near_send_sems.at[cell, p], near_recv_sems.at[cell, p], target,
+                group_sems.at[2], near_recv_sems.at[cell - 1, p], target,
             )
             for p in range(pieces)
         ]
 
-    near = {}
-    for d, e in ((2, 0), (0, 2), (2, 2)):
-        near[d * REACH + e] = near_copies(0, d * REACH + e, behind(d, e))
+    beside = (r, c + 1 - 2 * side)
+    near = {
+        2 * REACH: near_copies(0, 2 * REACH, behind(2, 0)),
+        2: near_copies(0, 2, behind(0, 2)),
+        2 * REACH + 2: near_copies(2 * REACH, 2 * REACH + 2, behind(0, 2)),
+    }
+    last, end = c >= cols - near_reach, c == cols - 1
+    around = {e: near_copies(e, 2 * REACH + e, behind(2, 0)) for e in (1, 2)}
+    first_to_end = near_copies(0, 1, (r, cols - 1))
     for d in (0, 2):
-        cell = d * REACH + 1
-        row, col = behind(d, 1)
-        near[cell] = near_copies(
-            (cell + 1) * (1 - side), cell, (jnp.where(passes, r, row), jnp.where(passes, c + 1, col))
-        )
+        near[d * REACH + 1] = near_copies(d * REACH + 2 * (1 - side), d * REACH + 1, beside)
     for e in range(REACH):
         near[REACH + e] = near_copies(2 * REACH * (1 - parity) + e, REACH + e, partner)
+
     chunks = [
         remote(
             up_send.at[j],
@@ -188,63 +247,50 @@
         for j in range(n_red)
     ]
     leaves = [
-        remote(leaf_send, leaf_buf.at[j], group_sems.at[2], own_sems.at[j // group], behind(0, REACH + j))
+        remote(leaf_send, leaf_buf.at[j], group_sems.at[3], own_sems.at[j // group], behind(0, REACH + j))
         for j in range(band)
     ]
     band_up = [
         remote(
             leaf_buf.at[pl.ds(j, n)], leaf_buf.at[pl.ds(2 * band + j, n)],
-            up_send_sems.at[j // group], up_recv_sems.at[j // group], behind(2, 0),
+            group_sems.at[3], up_recv_sems.at[j // group], behind(2, 0),
         )
         for j, n in spans
     ]
     band_across = [
         remote(
             leaf_buf.at[pl.ds(2 * band * (1 - parity) + j, n)], leaf_buf.at[pl.ds(band + j, n)],
-            across_send_sems.at[j // group], across_recv_sems.at[j // group], partner,
+            group_sems.at[3], group_sems.at[6], partner,
         )
         for j, n in spans
     ]
 
+    def known(target, stage, is_near=None):
+        below = place(*target) < mine
+        if stage == 0:
+            return below
+        close = near_column(target[1])
+        return jnp.logical_and(jnp.logical_not(below), close if stage == 1 else jnp.logical_not(close))
+
+    def start_all(copies, condition):
+        for copy in copies:
+            when(condition, copy.start)
+
     def sends(stage):
-        def column(e):
-            return c >= e if stage == 0 else c < e
-
+        if stage != 2:
+            start_all(near[2 * REACH], known(behind(2, 0), stage))
         for j in range(n_red):
-            up_by = first_red + j - c
-            if stage == 0:
-                known = up_by < 0
-            elif stage == 1:
-                known = jnp.logical_and(up_by > 0, up_by <= near_reach)
-            else:
-                known = up_by > near_reach
-            when(known, chunks[j].start)
+            target = (r, first_red + j)
+            when(jnp.logical_and(known(target, stage), target[1] != c), chunks[j].start)
         for j in range(band):
-            e = REACH + j
-            if stage != (1 if cols - e > near_reach else 2):
-                when(column(e), leaves[j].start)
-        if stage != 1:
-            for d in (0, 2):
-                for near_copy in near[d * REACH + 2]:
-                    when(column(2), near_copy.start)
+            when(known(behind(0, REACH + j), stage), leaves[j].start)
+        if stage != 2:
+            start_all(near[2], known(behind(0, 2), stage))
         if stage == 0:
-            for d in (0, 2):
-                for near_copy in near[d * REACH + 1]:
-                    when(direct, near_copy.start)
-        if stage != 2:
-            below = r >= 2
-            for near_copy in near[2 * REACH]:
-                when(below if stage == 0 else jnp.logical_not(below), near_copy.start)
-
-    higher = cols - 1 - c
-    close = jnp.minimum(near_reach, higher)
-    pl.semaphore_wait(barrier, r + rows * c + 1 - parity)
-    greet(near_sem, 0, 0, r - parity)
-    greet_columns(1, near_reach + 1, lambda e: c >= e, near_sem)
-    greet_columns(near_reach + 1, cols, lambda e: c >= e, far_sem)
+            start_all(near[1], direct)
+
     sends(0)
-    above = rows - 2 - r + parity + rows * close
-    when(above > 0, lambda: pl.semaphore_wait(near_sem, above))
+    when(n_near_above > 0, lambda: pl.semaphore_wait(near_sem, n_near_above))
     sends(1)
 
     for near_copy in near[REACH]:
@@ -263,15 +309,24 @@
         return dot(source, blocks[slot], ((1,), (0,)))
 
     total = term(0)
-    distant = rows * (higher - close)
-    when(distant > 0, lambda: pl.semaphore_wait(far_sem, distant))
+    wraps = known(behind(0, 2), 2)
+
+    def facing_arrived(pass_on):
+        for p in range(pieces):
+            near[2 * REACH][p].wait_recv()
+            if pass_on:
+                near[2 * REACH + 2][p].start()
+            when(direct, near[2 * REACH + 1][p].start)
+            when(even, near[REACH][p].start)
+
+    when(wraps, lambda: facing_arrived(False))
+    when(n_far_above > 0, lambda: pl.semaphore_wait(far_sem, n_far_above))
     sends(2)
-
     arrived = chunk_buf.at[pl.ds(1, cols - 1)]
 
-    @pl.when(is_red)
-    def _():
+    def reduce_chunks():
         pltpu.make_async_copy(arrived, arrived, group_sems.at[1]).wait()
+        when(n_region_above > 0, lambda: pl.semaphore_wait(region_sem, n_region_above))
         reduced = up_send[jnp.clip(c - first_red, 0, n_red - 1)].astype(F32)
         for e in range(1, cols):
             reduced = reduced + chunk_buf[e].astype(F32)
@@ -287,10 +342,14 @@
         cell = d * REACH + e
         for p in range(pieces):
             near[cell][p].wait_recv()
-            if (d, e) != (0, 0):
-                when(odd if d == 0 else even, near[REACH + e][p].start)
+            when(odd if d == 0 else even, near[REACH + e][p].start)
+            if d == 0:
+                when(last if e == 2 else end, around[e][p].start)
             if e == 2:
-                when(passes, near[cell - 1][p].start)
+                when(jnp.logical_and(passes, c != cols - 2), near[cell - 1][p].start)
+
+    when(is_red, reduce_chunks)
+    when(jnp.logical_not(wraps), lambda: facing_arrived(True))
 
     def own_groups(lo, hi):
         for g in range(lo, hi):
@@ -305,17 +364,33 @@
             near_copy.wait_recv()
         return term(cell)
 
-    own_groups(0, len(spans))
-    got(0, 2)
-    got(2, 2)
-    got(2, 0)
-    for g in range(len(spans)):
-        band_up[g].wait_recv()
-        when(even, band_across[g].start)
+    def up_groups():
+        for g in range(len(spans)):
+            band_up[g].wait_recv()
+            when(even, band_across[g].start)
+
+    def arrivals_last():
+        own_groups(0, len(spans))
+        got(0, 2)
+        when(end, lambda: got(0, 1))
+        up_groups()
+        got(2, 2)
+
+    def arrivals():
+        own_groups(0, 1)
+        start_all(near[2], wraps)
+        start_all(first_to_end, c == 0)
+        own_groups(1, len(spans))
+        got(0, 2)
+        got(2, 2)
+        up_groups()
+
+    when(last, arrivals_last)
+    when(jnp.logical_not(last), arrivals)
     for cell in (2 * REACH, 2, 2 * REACH + 2):
         total = total + term(cell)
     total = total + here(REACH)
-    got(0, 1)
+    when(jnp.logical_not(end), lambda: got(0, 1))
     total = total + term(1)
 
     pltpu.make_async_copy(region_buf, region_buf, group_sems.at[5]).wait()
@@ -330,8 +405,8 @@
         product = dot(coupling[slot], region, ((0,), (0,)))
         region_out = product if region_out is None else region_out + product
     leaf_out = dot(transfer_row[...], region_out.astype(BF16), ((0,), (0,)))
-    for g in range(len(spans)):
-        band_across[g].wait_recv()
+    mid_band = leaf_buf.at[pl.ds(band, band)]
+    pltpu.make_async_copy(mid_band, mid_band, group_sems.at[6]).wait()
     leaf_out = leaf_out + dot(
         couple[...].reshape(REACH * band * rank, rank),
         leaf_buf[...].reshape(REACH * band * rank, vecs),
@@ -344,14 +419,16 @@
     total = total + here(REACH + 1)
     out_ref[...] = total.astype(out_ref.dtype)
 
-    for copies in near.values():
-        for copy in copies:
-            copy.wait_send()
-    for copy in band_up + band_across:
-        copy.wait_send()
-
-    own_band = leaf_buf.at[pl.ds(0, band)]
-    pltpu.make_async_copy(own_band, own_band, group_sems.at[2]).wait()
+    def sent(cells):
+        view = table.at[pl.ds(0, cells)]
+        pltpu.make_async_copy(view, view, group_sems.at[2]).wait()
+
+    n_sent = table.shape[0] - 1
+    short = jnp.logical_or(c == near_reach - 1, c == cols - near_reach)
+    when(short, lambda: sent(n_sent - 1))
+    when(end, lambda: [sent(n_sent + 1), sent(1)])
+    when(jnp.logical_not(jnp.logical_or(short, end)), lambda: sent(n_sent))
+    pltpu.make_async_copy(leaf_buf, leaf_buf, group_sems.at[3]).wait()
 
     @pl.when(is_red)
     def _():
@@ -383,7 +460,7 @@
     rank = basis_col.shape[2]
     cells = near_blocks.shape[2]
     band = leaf_couple.shape[3]
-    n_red = cols // 2
+    n_red = cols // 4
     groups = min(band, 5)
     groups = -(-band // -(-band // groups))
     hbm = pl.BlockSpec(memory_space=pl.ANY)
@@ -411,14 +488,11 @@
             pltpu.VMEM((cols, rank // n_red, vecs), BF16),
             pltpu.VMEM((rows - REACH, n_red, rank // n_red, vecs), BF16),
             pltpu.SemaphoreType.DMA((11,)),
-            pltpu.SemaphoreType.DMA((cells, PIECES)),
-            pltpu.SemaphoreType.DMA((cells, PIECES)),
+            pltpu.SemaphoreType.DMA((cells - 1, PIECES)),
             pltpu.SemaphoreType.DMA((groups,)),
             pltpu.SemaphoreType.DMA((groups,)),
-            pltpu.SemaphoreType.DMA((groups,)),
-            pltpu.SemaphoreType.DMA((groups,)),
-            pltpu.SemaphoreType.DMA((groups,)),
-            pltpu.SemaphoreType.DMA((6,)),
+            pltpu.SemaphoreType.DMA((7,)),
+            pltpu.SemaphoreType.REGULAR,
             pltpu.SemaphoreType.REGULAR,
             pltpu.SemaphoreType.REGULAR,
         ],

time: 20.3 us -> 19.8 us (0.975)
  the two profiles are of different devices: /device:TPU:27 before, /device:TPU:25 now
where the time goes in v3:
time: 19.8 us; the launch traced here: 19.6 us
  Pallas kernels  18.3 us (92%)
  between operations  0.66 us (3%)
  local copies, waits for them, and re-layouts  0.64 us (3%)
    pallas_call x1, Pallas kernels, per_device(): pl.pallas_call(functools.partial(kernel, rows, cols), out_shape=pltpu.VME...  18.3 us
    unnamed x1, local copies, waits for them, and re-layouts  0.64 us

profile of v3, /device:TPU:25, one launch (start us, length us, event | category | flops | bytes accessed | tf_op | source)
XLA Modules:
  0.0 19.6 jit_solution(15322029475842923101)
XLA Ops:
  0.7 18.3 %shard_map.109 = bf16[128,384]{1,0:T(8,128)(2,1)S(1)} custom-call(s32[9]{0:T(128)} %bitcast.20, s32[1,1]{1,0:T(1,128)S(6)} %copy.14.count_hbm, s32[4]{0:T(128)} %bitcast.21, bf16[128,384]{1,0:T(8,128)(2,1)} %bitcast.14, bf16[9,384,384]{2,1,0:T(8,128)(2,1)} %bitcast.12, bf16[64,384]{1,0:T(8,128)(2,1)} %bitcast.16, bf16[64,64]{1,0:T(8,128)(2,1)} %bitcast.18, ...), custom_call_target="tpu_custom_call" | custom-call | tf_op jit(solution)/shard_map/pallas_call | solution.py:467
  19.0 0.6 %copy.13 = bf16[1,1,128,384]{3,2,1,0:T(8,128)(2,1)} copy(bf16[1,1,128,384]{3,2,1,0:T(8,128)(2,1)S(1)} %bitcast.11) | data formatting | bytes 196608

commit v4 on v3

--- a/solution.py
+++ b/solution.py
@@ -58,6 +58,8 @@
     near_sem,
     far_sem,
     region_sem,
+    facing_sem,
+    go_sem,
 ):
     r, c = lax.axis_index("row"), lax.axis_index("col")
     parity = lax.rem(r, 2)
@@ -123,7 +125,7 @@
 
     kinds = [
         (cols - 1, to_row, near_column),
-        (2 if rows > 4 else 1, to_facing, lambda col: one),
+        (2 if rows > 4 else 1, to_facing, None),
         (far_rows * cols, to_targets, None),
         (far_rows * n_red, to_reducers, None),
     ]
@@ -140,9 +142,11 @@
                     when(jnp.logical_and(valid, place(*device) > mine), functools.partial(greet, barrier, device))
                     return
                 below = jnp.logical_and(valid, place(*device) < mine)
+                if which is to_facing:
+                    when(below, functools.partial(greet, facing_sem, device))
+                if which is to_reducers:
+                    when(below, functools.partial(greet, region_sem, device))
                 if is_near is None:
-                    if which is to_reducers:
-                        when(below, functools.partial(greet, region_sem, device))
                     return
                 close = is_near(device[1])
                 when(jnp.logical_and(below, close), functools.partial(greet, near_sem, device))
@@ -162,7 +166,10 @@
                 above = place(*device) > mine
                 no = jnp.logical_not(one)
                 if is_near is None:
-                    found = (jnp.logical_not(above), no, no, above if which is to_targets else no)
+                    found = (
+                        jnp.logical_not(above), no, no,
+                        above if which is to_targets else no, above if which is to_facing else no,
+                    )
                 else:
                     close = is_near(device[1])
                     found = (
@@ -170,6 +177,7 @@
                         jnp.logical_and(above, close),
                         jnp.logical_and(above, jnp.logical_not(close)),
                         no,
+                        no,
                     )
                 return tuple(n + jnp.where(jnp.logical_and(valid, f), 1, 0) for n, f in zip(numbers, found))
 
@@ -183,7 +191,7 @@
     greet(barrier, (r + 1 - 2 * parity, c))
     greet_all(False)
     zero = jnp.int32(0)
-    n_below, n_near_above, n_far_above, n_region_above = count_all((jnp.int32(1), zero, zero, zero))
+    n_below, n_near_above, n_far_above, n_region_above, n_facing_above = count_all((jnp.int32(1), zero, zero, zero, zero))
 
     for load in loads[3:]:
         load.start()
@@ -247,7 +255,7 @@
         for j in range(n_red)
     ]
     leaves = [
-        remote(leaf_send, leaf_buf.at[j], group_sems.at[3], own_sems.at[j // group], behind(0, REACH + j))
+        remote(leaf_send, leaf_buf.at[j], group_sems.at[7], own_sems.at[j // group], behind(0, REACH + j))
         for j in range(band)
     ]
     band_up = [
@@ -277,8 +285,6 @@
             when(condition, copy.start)
 
     def sends(stage):
-        if stage != 2:
-            start_all(near[2 * REACH], known(behind(2, 0), stage))
         for j in range(n_red):
             target = (r, first_red + j)
             when(jnp.logical_and(known(target, stage), target[1] != c), chunks[j].start)
@@ -288,8 +294,12 @@
             start_all(near[2], known(behind(0, 2), stage))
         if stage == 0:
             start_all(near[1], direct)
+        if stage == 0:
+            start_all(near[2 * REACH], known(behind(2, 0), stage))
 
     sends(0)
+    when(n_facing_above > 0, lambda: pl.semaphore_wait(facing_sem, n_facing_above))
+    start_all(near[2 * REACH], jnp.logical_not(known(behind(2, 0), 0)))
     when(n_near_above > 0, lambda: pl.semaphore_wait(near_sem, n_near_above))
     sends(1)
 
@@ -300,10 +310,16 @@
 
     count = count_ref[0, 0]
 
+    sources = [source_ref[s] for s in range(source_ref.shape[0])]
+    slots = []
+    for cell in range(len(sources)):
+        slot = jnp.int32(0)
+        for s, source in enumerate(sources):
+            slot = jnp.where(source == cell, s, slot)
+        slots.append(slot)
+
     def term(cell):
-        slot = jnp.int32(0)
-        for s in range(source_ref.shape[0]):
-            slot = jnp.where(source_ref[s] == cell, s, slot)
+        slot = slots[cell]
         source = table[cell]
         source = jnp.where(slot < count, source, jnp.zeros_like(source))
         return dot(source, blocks[slot], ((1,), (0,)))
@@ -322,6 +338,25 @@
     when(wraps, lambda: facing_arrived(False))
     when(n_far_above > 0, lambda: pl.semaphore_wait(far_sem, n_far_above))
     sends(2)
+
+    follows = jnp.logical_and(c >= near_reach, c < 2 * near_reach)
+    own_band = leaf_buf.at[pl.ds(0, band)]
+
+    def leaves_sent():
+        pltpu.make_async_copy(own_band, own_band, group_sems.at[7]).wait()
+
+    def release():
+        leaves_sent()
+        greet(go_sem, (r, lax.rem(c + cols - near_reach, cols)))
+
+    when(follows, release)
+
+    def wrap():
+        pl.semaphore_wait(go_sem, 1)
+        start_all(near[2], one)
+        start_all(first_to_end, c == 0)
+
+    when(c == 1, wrap)
     arrived = chunk_buf.at[pl.ds(1, cols - 1)]
 
     def reduce_chunks():
@@ -369,28 +404,25 @@
             band_up[g].wait_recv()
             when(even, band_across[g].start)
 
-    def arrivals_last():
-        own_groups(0, len(spans))
-        got(0, 2)
-        when(end, lambda: got(0, 1))
-        up_groups()
-        got(2, 2)
-
-    def arrivals():
-        own_groups(0, 1)
-        start_all(near[2], wraps)
-        start_all(first_to_end, c == 0)
-        own_groups(1, len(spans))
-        got(0, 2)
-        got(2, 2)
-        up_groups()
-
-    when(last, arrivals_last)
-    when(jnp.logical_not(last), arrivals)
-    for cell in (2 * REACH, 2, 2 * REACH + 2):
+    own_groups(0, 1)
+    when(c == 0, wrap)
+    own_groups(1, len(spans))
+    got(0, 2)
+    when(end, lambda: got(0, 1))
+
+    def from_beside():
+        got(0, 1)
+        got(2, 1)
+
+    when(passes, from_beside)
+    when(jnp.logical_not(last), lambda: got(2, 2))
+    for cell in (2 * REACH, 2):
         total = total + term(cell)
+    up_groups()
+    when(last, lambda: got(2, 2))
+    total = total + term(2 * REACH + 2)
     total = total + here(REACH)
-    when(jnp.logical_not(end), lambda: got(0, 1))
+    when(jnp.logical_and(direct, jnp.logical_not(end)), lambda: got(0, 1))
     total = total + term(1)
 
     pltpu.make_async_copy(region_buf, region_buf, group_sems.at[5]).wait()
@@ -413,7 +445,7 @@
         ((0,), (0,)),
     )
     total = total + dot(leaf_out.astype(BF16), basis_row[...], ((0,), (0,)))
-    got(2, 1)
+    when(direct, lambda: got(2, 1))
     total = total + term(2 * REACH + 1)
     total = total + here(REACH + 2)
     total = total + here(REACH + 1)
@@ -428,7 +460,9 @@
     when(short, lambda: sent(n_sent - 1))
     when(end, lambda: [sent(n_sent + 1), sent(1)])
     when(jnp.logical_not(jnp.logical_or(short, end)), lambda: sent(n_sent))
-    pltpu.make_async_copy(leaf_buf, leaf_buf, group_sems.at[3]).wait()
+    upper_bands = leaf_buf.at[pl.ds(band, 2 * band)]
+    pltpu.make_async_copy(upper_bands, upper_bands, group_sems.at[3]).wait()
+    when(jnp.logical_not(follows), leaves_sent)
 
     @pl.when(is_red)
     def _():
@@ -491,7 +525,9 @@
             pltpu.SemaphoreType.DMA((cells - 1, PIECES)),
             pltpu.SemaphoreType.DMA((groups,)),
             pltpu.SemaphoreType.DMA((groups,)),
-            pltpu.SemaphoreType.DMA((7,)),
+            pltpu.SemaphoreType.DMA((8,)),
+            pltpu.SemaphoreType.REGULAR,
+            pltpu.SemaphoreType.REGULAR,
             pltpu.SemaphoreType.REGULAR,
             pltpu.SemaphoreType.REGULAR,
             pltpu.SemaphoreType.REGULAR,

time: 19.8 us -> 18.8 us (0.949)
  the two profiles are of different devices: /device:TPU:25 before, /device:TPU:27 now
where the time goes in v4:
time: 18.8 us; the launch traced here: 18.6 us
  Pallas kernels  17.3 us (92%)
  between operations  0.66 us (4%)
  local copies, waits for them, and re-layouts  0.64 us (3%)
    pallas_call x1, Pallas kernels, per_device(): pl.pallas_call(functools.partial(kernel, rows, cols), out_shape=pltpu.VME...  17.3 us
    unnamed x1, local copies, waits for them, and re-layouts  0.64 us

profile of v4, /device:TPU:27, one launch (start us, length us, event | category | flops | bytes accessed | tf_op | source)
XLA Modules:
  0.0 18.6 jit_solution(13515602317629702247)
XLA Ops:
  0.7 17.3 %shard_map.109 = bf16[128,384]{1,0:T(8,128)(2,1)S(1)} custom-call(s32[9]{0:T(128)} %bitcast.20, s32[1,1]{1,0:T(1,128)S(6)} %copy.14.count_hbm, s32[4]{0:T(128)} %bitcast.21, bf16[128,384]{1,0:T(8,128)(2,1)} %bitcast.14, bf16[9,384,384]{2,1,0:T(8,128)(2,1)} %bitcast.12, bf16[64,384]{1,0:T(8,128)(2,1)} %bitcast.16, bf16[64,64]{1,0:T(8,128)(2,1)} %bitcast.18, ...), custom_call_target="tpu_custom_call" | custom-call | tf_op jit(solution)/shard_map/pallas_call | solution.py:501
  18.0 0.6 %copy.13 = bf16[1,1,128,384]{3,2,1,0:T(8,128)(2,1)} copy(bf16[1,1,128,384]{3,2,1,0:T(8,128)(2,1)S(1)} %bitcast.11) | data formatting | bytes 196608

commit v5 on v4

--- a/solution.py
+++ b/solution.py
@@ -78,7 +78,7 @@
             act()
 
     loads = [
-        pltpu.make_async_copy(src, dst, local_sems.at[i])
+        pltpu.make_async_copy(src, dst, local_sems.at[min(i, 3)])
         for i, (src, dst) in enumerate(
             [
                 (vectors_hbm, table.at[0]),
@@ -225,7 +225,9 @@
         return [
             remote(
                 table.at[source, pl.ds(p * part, part)], table.at[cell, pl.ds(p * part, part)],
-                group_sems.at[2], near_recv_sems.at[cell - 1, p], target,
+                group_sems.at[2],
+                group_sems.at[5 + cell] if REACH <= cell < 2 * REACH else near_recv_sems.at[cell - 1 - (REACH if cell > 2 else 0), p],
+                target,
             )
             for p in range(pieces)
         ]
@@ -381,7 +383,10 @@
             if d == 0:
                 when(last if e == 2 else end, around[e][p].start)
             if e == 2:
-                when(jnp.logical_and(passes, c != cols - 2), near[cell - 1][p].start)
+                on = jnp.logical_and(passes, c != cols - 2)
+                when(jnp.logical_and(on, odd) if d == 0 else on, near[cell - 1][p].start)
+        if (d, e) == (2, 2):
+            start_all(near[1], jnp.logical_and(on, even))
 
     when(is_red, reduce_chunks)
     when(jnp.logical_not(wraps), lambda: facing_arrived(True))
@@ -395,8 +400,8 @@
             when(odd, band_across[g].start)
 
     def here(cell):
-        for near_copy in near[cell]:
-            near_copy.wait_recv()
+        view = table.at[cell]
+        pltpu.make_async_copy(view, view, group_sems.at[5 + cell]).wait()
         return term(cell)
 
     def up_groups():
@@ -422,8 +427,8 @@
     when(last, lambda: got(2, 2))
     total = total + term(2 * REACH + 2)
     total = total + here(REACH)
-    when(jnp.logical_and(direct, jnp.logical_not(end)), lambda: got(0, 1))
-    total = total + term(1)
+    inner = jnp.logical_and(direct, jnp.logical_not(end))
+    when(jnp.logical_and(inner, odd), lambda: got(0, 1))
 
     pltpu.make_async_copy(region_buf, region_buf, group_sems.at[5]).wait()
     rank, vecs = leaf_buf.shape[1:]
@@ -448,6 +453,8 @@
     when(direct, lambda: got(2, 1))
     total = total + term(2 * REACH + 1)
     total = total + here(REACH + 2)
+    when(jnp.logical_and(inner, even), lambda: got(0, 1))
+    total = total + term(1)
     total = total + here(REACH + 1)
     out_ref[...] = total.astype(out_ref.dtype)
 
@@ -521,11 +528,11 @@
             pltpu.VMEM((REACH * band, rank, vecs), BF16),
             pltpu.VMEM((cols, rank // n_red, vecs), BF16),
             pltpu.VMEM((rows - REACH, n_red, rank // n_red, vecs), BF16),
-            pltpu.SemaphoreType.DMA((11,)),
-            pltpu.SemaphoreType.DMA((cells - 1, PIECES)),
+            pltpu.SemaphoreType.DMA((4,)),
+            pltpu.SemaphoreType.DMA((cells - 1 - REACH, PIECES)),
             pltpu.SemaphoreType.DMA((groups,)),
             pltpu.SemaphoreType.DMA((groups,)),
-            pltpu.SemaphoreType.DMA((8,)),
+            pltpu.SemaphoreType.DMA((8 + REACH,)),
             pltpu.SemaphoreType.REGULAR,
             pltpu.SemaphoreType.REGULAR,
             pltpu.SemaphoreType.REGULAR,

time: 18.8 us -> 18.6 us (0.989)
  no operation moved by 1% of the time
where the time goes in v5:
time: 18.6 us; the launch traced here: 18.5 us
  Pallas kernels  17.2 us (92%)
  between operations  0.66 us (4%)
  local copies, waits for them, and re-layouts  0.64 us (3%)
    pallas_call x1, Pallas kernels, per_device(): pl.pallas_call(functools.partial(kernel, rows, cols), out_shape=pltpu.VME...  17.2 us
    unnamed x1, local copies, waits for them, and re-layouts  0.64 us

profile of v5, /device:TPU:27, one launch (start us, length us, event | category | flops | bytes accessed | tf_op | source)
XLA Modules:
  0.0 18.5 jit_solution(14224679852351024421)
XLA Ops:
  0.7 17.2 %shard_map.109 = bf16[128,384]{1,0:T(8,128)(2,1)S(1)} custom-call(s32[9]{0:T(128)} %bitcast.20, s32[1,1]{1,0:T(1,128)S(6)} %copy.14.count_hbm, s32[4]{0:T(128)} %bitcast.21, bf16[128,384]{1,0:T(8,128)(2,1)} %bitcast.14, bf16[9,384,384]{2,1,0:T(8,128)(2,1)} %bitcast.12, bf16[64,384]{1,0:T(8,128)(2,1)} %bitcast.16, bf16[64,64]{1,0:T(8,128)(2,1)} %bitcast.18, ...), custom_call_target="tpu_custom_call" | custom-call | tf_op jit(solution)/shard_map/pallas_call | solution.py:508
  17.8 0.6 %copy.13 = bf16[1,1,128,384]{3,2,1,0:T(8,128)(2,1)} copy(bf16[1,1,128,384]{3,2,1,0:T(8,128)(2,1)S(1)} %bitcast.11) | data formatting | bytes 196608

commit v6 on v5

--- a/solution.py
+++ b/solution.py
@@ -419,8 +419,8 @@
         got(0, 1)
         got(2, 1)
 
+    when(jnp.logical_not(last), lambda: got(2, 2))
     when(passes, from_beside)
-    when(jnp.logical_not(last), lambda: got(2, 2))
     for cell in (2 * REACH, 2):
         total = total + term(cell)
     up_groups()

time: 18.6 us -> 18.6 us (level)
  no operation moved by 1% of the time
where the time goes in v6:
time: 18.6 us; the launch traced here: 18.5 us
  Pallas kernels  17.2 us (92%)
  between operations  0.66 us (4%)
  local copies, waits for them, and re-layouts  0.64 us (3%)
    pallas_call x1, Pallas kernels, per_device(): pl.pallas_call(functools.partial(kernel, rows, cols), out_shape=pltpu.VME...  17.2 us
    unnamed x1, local copies, waits for them, and re-layouts  0.64 us

profile of v6, /device:TPU:27, one launch (start us, length us, event | category | flops | bytes accessed | tf_op | source)
XLA Modules:
  0.0 18.5 jit_solution(8383572490990650622)
XLA Ops:
  0.7 17.2 %shard_map.109 = bf16[128,384]{1,0:T(8,128)(2,1)S(1)} custom-call(s32[9]{0:T(128)} %bitcast.20, s32[1,1]{1,0:T(1,128)S(6)} %copy.14.count_hbm, s32[4]{0:T(128)} %bitcast.21, bf16[128,384]{1,0:T(8,128)(2,1)} %bitcast.14, bf16[9,384,384]{2,1,0:T(8,128)(2,1)} %bitcast.12, bf16[64,384]{1,0:T(8,128)(2,1)} %bitcast.16, bf16[64,64]{1,0:T(8,128)(2,1)} %bitcast.18, ...), custom_call_target="tpu_custom_call" | custom-call | tf_op jit(solution)/shard_map/pallas_call | solution.py:508
  17.8 0.6 %copy.13 = bf16[1,1,128,384]{3,2,1,0:T(8,128)(2,1)} copy(bf16[1,1,128,384]{3,2,1,0:T(8,128)(2,1)S(1)} %bitcast.11) | data formatting | bytes 196608
